TPU v7x, 32 devices: a whole 2x2x4 slice. The times are simulated.
32 devices in a mesh: rows: 8 (over z, y), cols: 4 (over x, core).
Axes of the slice: x: 2, y: 2, z: 4, core: 2. Of those that a mesh axis runs over, the one named last changes fastest.
Arguments:
- gradients: float32 [32, 128, 4096], P(None, 'rows', 'cols'), may hold values from -6 to 6
- momentum: float32 [32, 128, 4096], P(None, 'rows', 'cols'), may hold values from -6 to 6
- weights: float32 [32, 128, 4096], P(None, 'rows', 'cols'), may hold values from -0.1875 to 0.1875
Outputs:
- new_weights: float32 [32, 128, 4096], P(None, 'rows', 'cols')
- new_momentum: float32 [32, 128, 4096], P(None, 'rows', 'cols')
All inputs are finite; a program needn't handle non-finite values.
Results may differ from a plain program's by a relative error of at most 0.0003.
Values sent between devices are 32-bit elements.
A program may use at most 64 MiB of HBM per device.

v0:
```python
import jax
import jax.numpy as jnp
from jax import lax
from jax.sharding import PartitionSpec as P

ITERS = 4


hold_rate = 0.8
learn_rate = 0.8
decay_rate = 0.1


def mul(a, b):
    return jnp.einsum("mij,mjk->mik", a, b, precision=lax.Precision.HIGHEST)


def local(gradients, momentum, weights):
    new_momentum = hold_rate * momentum + gradients
    whole = lax.all_to_all(new_momentum, "rows", split_axis=0, concat_axis=1, tiled=True)
    gram = jnp.einsum("mik,mjk->mij", whole, whole, precision=lax.Precision.HIGHEST)
    gram = lax.psum(gram, "cols")
    eye = jnp.eye(gram.shape[-1], dtype=jnp.float32)
    total = jnp.sum(gram * eye, axis=(1, 2), keepdims=True)
    scale = lax.rsqrt(total + 1e-06)
    gram = gram * scale * scale
    chain = scale * eye
    for step in range(ITERS):
        factor = 3.4445 * eye - 4.775 * gram + 2.0315 * mul(gram, gram)
        chain = mul(factor, chain)
        if step < ITERS - 1:
            gram = mul(factor, mul(gram, factor))
    iterate = mul(chain, whole)
    back = lax.all_to_all(iterate, "rows", split_axis=1, concat_axis=0, tiled=True)
    new_weights = (1.0 - learn_rate * decay_rate) * weights - learn_rate * back
    return (new_weights, new_momentum)


def solution(mesh):
    placed = (P(None, "rows", "cols"), P(None, "rows", "cols"), P(None, "rows", "cols"))
    return jax.shard_map(
        local,
        mesh=mesh,
        in_specs=placed,
        out_specs=(P(None, "rows", "cols"), P(None, "rows", "cols")),
        check_vma=False,
    )
```

profile of v0, /device:TPU:0, one launch (start us, length us, event | category | flops | bytes accessed | tf_op | source)
XLA Modules:
  0.0 178.0 jit_solution(10635801916381420988)
XLA Ops:
  7.2 0.0 all-reduce.2.cloned.1.call-start
  7.2 2.7 %multiply_add_fusion = f32[32,16,1024]{2,1,0:T(8,128)S(1)} fusion(f32[32,16,1024]{2,1,0:T(8,128)} %param.3, f32[32,16,1024]{2,1,0:T(8,128)} %param.4), kind=kLoop, calls=%fused_computation.1 | loop fusion | flops 1048576 | bytes 6291456 | tf_op jit(solution)/shard_map/add | solution.py:19
  9.9 0.0 copy-start
  9.9 55.8 %all_to_all.27 = f32[32,16,1024]{2,1,0:T(8,128)S(1)} all-to-all(f32[32,16,1024]{2,1,0:T(8,128)S(1)} %multiply_add_fusion), channel_id=1, replica_groups=mesh['rows'=8,'cols'=4] {'rows'}, dimensions={0} | all-to-all | bytes 4194304 | tf_op jit(solution)/shard_map/all_to_all | solution.py:20
  65.7 0.0 copy-done
  65.7 0.1 copy.7
  65.8 2.8 %fusion.13 = f32[4,128,128]{2,1,0:T(8,128)} fusion(f32[4,128,1024]{2,1,0:T(8,128)S(1)} %bitcast.37), kind=kOutput, calls=%fused_computation.24 | convolution fusion | flops 805306368 | bytes 2359296 | tf_op jit(solution)/shard_map/mik,mjk->mij/dot_general | solution.py:21
  68.6 0.0 all-reduce.2.cloned.1.call-update
  68.6 33.4 %all-reduce.2.cloned.1.call-done = f32[4,128,128]{2,1,0:T(8,128)} async-done(((f32[4,128,128]{2,1,0:T(8,128)}), f32[4,128,128]{2,1,0:T(8,128)}) %all-reduce.2.cloned.1.call-update) | async-done | bytes 262160 | tf_op jit(solution)/shard_map/psum | solution.py:22
  102.0 1.1 multiply_reduce_fusion
  103.1 1.6 fusion.3
  104.7 0.4 fusion.4
  105.2 1.4 fusion.6
  106.5 0.4 fusion.14
  106.9 0.4 fusion.2
  107.3 0.4 fusion.15
  107.7 0.4 fusion.19
  108.1 0.4 fusion.16
  108.5 0.4 fusion.1
  108.9 0.4 fusion.17
  109.3 0.4 fusion.20
  109.7 0.4 fusion.18
  110.1 0.4 fusion
  110.5 0.4 fusion.21
  110.9 1.9 %fusion.22 = f32[4,128,1024]{2,1,0:T(8,128)S(1)} fusion(f32[4,128,128]{2,1,0:T(8,128)S(1)} %fusion.21, f32[4,128,1024]{2,1,0:T(8,128)S(1)} %bitcast.38), kind=kOutput, calls=%fused_computation.33 | convolution fusion | flops 805306368 | bytes 4456448 | tf_op jit(solution)/shard_map/mij,mjk->mik/dot_general | solution.py:15
  112.8 1.4 copy.8
  114.2 53.0 %all_to_all.28 = f32[4,128,1024]{2,0,1:T(4,128)S(1)} all-to-all(f32[4,128,1024]{2,0,1:T(4,128)S(1)} %copy.8), channel_id=1, replica_groups=mesh['rows'=8,'cols'=4] {'rows'}, dimensions={1} | all-to-all | bytes 4194304 | tf_op jit(solution)/shard_map/all_to_all | solution.py:34
  167.2 0.6 broadcast_multiply_fusion
  167.8 0.0 copy-start.1
  167.8 1.2 copy.9
  169.0 0.4 copy-done.1
  169.4 1.8 bitcast_subtract_fusion
  (3 shorter events, 0.0 us)
Async XLA Ops:
  7.2 94.8 %all-reduce.2.cloned.1.call-start = ((), (), s32[]{:S(2)}) async-start(), calls=%async_computation.2 | async-start | bytes 524288 | tf_op jit(solution)/shard_map/psum | solution.py:22
  9.9 55.8 %copy-start = (f32[32,16,1024]{2,1,0:T(8,128)}, f32[32,16,1024]{2,1,0:T(8,128)S(1)}, u32[]{:S(2)}) copy-start(f32[32,16,1024]{2,1,0:T(8,128)S(1)} %multiply_add_fusion) | copy-start | bytes 6291460
  167.8 1.6 copy-start.1
Sparse Core Ops, SparseCore 0:
  68.7 33.2 all-reduce.1
where the time goes:
time: 178 us
  blocking collectives  109 us (61%)
  waiting for transfers between devices  33.4 us (19%)
  between operations  14.2 us (8%)
  matrix products  12.4 us (7%)
  other arithmetic  6.1 us (3%)
  local copies, waits for them, and re-layouts  3.07 us (2%)
    all_to_all x1, blocking collectives, local(): lax.all_to_all(new_momentum, 'rows', split_axis=0, concat_axis=1, tiled=T...  55.8 us
    all_to_all x1, blocking collectives, local(): lax.all_to_all(iterate, 'rows', split_axis=1, concat_axis=0, tiled=True)  53 us
    psum x1, waiting for transfers between devices, local(): gram = lax.psum(gram, 'cols')  33.4 us
    dot_general x15, matrix products, mul(): return jnp.einsum('mij,mjk->mik', a, b, precision=lax.Precision.HIGHEST)  9.65 us
  transfers between devices with their start and end apart: 1, of which 1 were waited for; matrix products, arithmetic and copies ran while one was open for 0% of the time, Pallas kernels for 0%

commit v1 on v0

v1 whole, which is shorter than its diff:
```python
import functools

import jax
import jax.numpy as jnp
from jax import lax
from jax.experimental import pallas as pl
from jax.experimental.pallas import tpu as pltpu
from jax.sharding import PartitionSpec as P

ITERS = 4


hold_rate = 0.8
learn_rate = 0.8
decay_rate = 0.1

MESH = pl.DeviceIdType.MESH


def split(x):
    high = x.astype(jnp.bfloat16)
    return high, (x - high.astype(jnp.float32)).astype(jnp.bfloat16)


def dot(a, b):
    return jnp.dot(a, b, preferred_element_type=jnp.float32)


def mul(a, b):
    side = b.shape[1]
    ah, al = split(a)
    bh, bl = split(b)
    right = jnp.concatenate([bh, bl], axis=1)
    out = dot(jnp.concatenate([ah, al], axis=1), jnp.concatenate([right, right], axis=0))
    return out[:, :side] + out[:, side:]


def gram_of(block, side, wide, tile):
    total = None
    for at in range(0, wide, tile):
        high, low = split(block[:, :, at : at + tile].reshape(side, tile))
        both = jnp.concatenate([high, low], axis=0)
        part = lax.dot_general(high, both, (((1,), (1,)), ((), ())), preferred_element_type=jnp.float32)
        total = part if total is None else total + part
    cross = total[:, side:]
    return total[:, :side] + cross + cross.T


def chain_of(gram):
    side = gram.shape[0]
    eye = (
        lax.broadcasted_iota(jnp.int32, (side, side), 0) == lax.broadcasted_iota(jnp.int32, (side, side), 1)
    ).astype(jnp.float32)
    total = jnp.sum(gram * eye, axis=(0, 1), keepdims=True)
    scale = lax.rsqrt(total + 1e-06)
    gram = gram * scale * scale
    chain = None
    for step in range(ITERS):
        factor = 3.4445 * eye - 4.775 * gram + 2.0315 * mul(gram, gram)
        chain = factor if chain is None else mul(factor, chain)
        if step < ITERS - 1:
            gram = mul(factor, mul(gram, factor))
    return chain * scale


def kernel(n, c, nm_ref, w_ref, out_ref, seen, grams, sent, back, w_buf,
           load_sem, own_sem, s1, r1, sg, rg, s2, r2, out_sem):
    _, per, b, wide = nm_ref.shape
    side = n * b
    me, my = lax.axis_index("rows"), lax.axis_index("cols")

    own = [pltpu.make_async_copy(nm_ref.at[me, j], seen.at[j, me], own_sem.at[j]) for j in range(per)]
    for copy in own:
        copy.start()
    load = pltpu.make_async_copy(w_ref, w_buf, load_sem)
    load.start()

    barrier = pltpu.get_barrier_semaphore()
    for k in range(1, n):
        pl.semaphore_signal(barrier, inc=1, device_id={"rows": lax.rem(me + k, n)}, device_id_type=MESH)
    for k in range(1, c):
        pl.semaphore_signal(barrier, inc=1, device_id={"cols": lax.rem(my + k, c)}, device_id_type=MESH)
    pl.semaphore_wait(barrier, n - 1 + c - 1)

    def there(j, k):
        to = lax.rem(me + k, n)
        return pltpu.make_async_remote_copy(
            src_ref=nm_ref.at[to, j], dst_ref=seen.at[j, me],
            send_sem=s1.at[j, k], recv_sem=r1.at[j, k],
            device_id={"rows": to}, device_id_type=MESH)

    def home(j, k):
        to = lax.rem(me + k, n)
        return pltpu.make_async_remote_copy(
            src_ref=sent.at[j, to], dst_ref=back.at[j, me],
            send_sem=s2.at[j, k], recv_sem=r2.at[j, k],
            device_id={"rows": to}, device_id_type=MESH)

    def across(j, k):
        return pltpu.make_async_remote_copy(
            src_ref=grams.at[j, my], dst_ref=grams.at[j, my],
            send_sem=sg.at[j, k], recv_sem=rg.at[j, k],
            device_id={"cols": lax.rem(my + k, c)}, device_id_type=MESH)

    for j in range(per):
        for k in range(1, n):
            there(j, k).start()

    tile = min(256, wide)

    def gram(j):
        own[j].wait()
        for k in range(1, n):
            there(j, k).wait_recv()
        grams[j, my] = gram_of(seen[j], side, wide, tile)
        for k in range(1, c):
            across(j, k).start()

    def step(j):
        for k in range(1, c):
            across(j, k).wait_recv()
        total = grams[j, 0]
        for k in range(1, c):
            total = total + grams[j, k]
        high, low = split(chain_of(total))
        left = jnp.concatenate([high, low], axis=1)
        for at in range(0, wide, tile):
            xh, xl = split(seen[j, :, :, at : at + tile].reshape(side, tile))
            part = dot(left, jnp.concatenate([xh, xh], axis=0)) + dot(high, xl)
            sent[j, :, :, at : at + tile] = part.reshape(n, b, tile)
        for k in range(1, n):
            home(j, k).start()
        back[j, me] = sent[j, me]

    def finish(j):
        for k in range(1, n):
            home(j, k).wait_recv()
        w_buf[:, j] = (1.0 - learn_rate * decay_rate) * w_buf[:, j] - learn_rate * back[j]
        pltpu.make_async_copy(w_buf.at[:, j], out_ref.at[:, j], out_sem.at[j]).start()

    gram(0)
    for j in range(per):
        if j + 1 < per:
            gram(j + 1)
        step(j)
    load.wait()
    for j in range(per):
        finish(j)
    for j in range(per):
        for k in range(1, n):
            there(j, k).wait_send()
            home(j, k).wait_send()
        for k in range(1, c):
            across(j, k).wait_send()
        pltpu.make_async_copy(w_buf.at[:, j], out_ref.at[:, j], out_sem.at[j]).wait()


def exchange_in_kernel(n, c, new_momentum, weights):
    mats, b, wide = weights.shape
    per, side = mats // n, n * b
    shape = (n, per, b, wide)
    dma = pltpu.SemaphoreType.DMA
    f32 = jnp.float32
    out = pl.pallas_call(
        functools.partial(kernel, n, c),
        out_shape=jax.ShapeDtypeStruct(shape, f32),
        in_specs=[pl.BlockSpec(memory_space=pl.ANY)] * 2,
        out_specs=pl.BlockSpec(memory_space=pl.ANY),
        scratch_shapes=[
            pltpu.VMEM((per, n, b, wide), f32),
            pltpu.VMEM((per, c, side, side), f32),
            pltpu.VMEM((per, n, b, wide), f32),
            pltpu.VMEM((per, n, b, wide), f32),
            pltpu.VMEM((n, per, b, wide), f32),
            dma, dma((per,)),
            dma((per, n)), dma((per, n)),
            dma((per, c)), dma((per, c)),
            dma((per, n)), dma((per, n)),
            dma((per,)),
        ],
        compiler_params=pltpu.CompilerParams(
            collective_id=0, has_side_effects=True, vmem_limit_bytes=40 * 2**20
        ),
    )(new_momentum.reshape(shape), weights.reshape(shape))
    return out.reshape(weights.shape)


def product(a, b):
    return jnp.einsum("mij,mjk->mik", a, b, precision=lax.Precision.HIGHEST)


def exchange_in_xla(new_momentum, weights):
    whole = lax.all_to_all(new_momentum, "rows", split_axis=0, concat_axis=1, tiled=True)
    gram = jnp.einsum("mik,mjk->mij", whole, whole, precision=lax.Precision.HIGHEST)
    gram = lax.psum(gram, "cols")
    eye = jnp.eye(gram.shape[-1], dtype=jnp.float32)
    total = jnp.sum(gram * eye, axis=(1, 2), keepdims=True)
    scale = lax.rsqrt(total + 1e-06)
    gram = gram * scale * scale
    chain = scale * eye
    for step in range(ITERS):
        factor = 3.4445 * eye - 4.775 * gram + 2.0315 * product(gram, gram)
        chain = product(factor, chain)
        if step < ITERS - 1:
            gram = product(factor, product(gram, factor))
    iterate = product(chain, whole)
    back = lax.all_to_all(iterate, "rows", split_axis=1, concat_axis=0, tiled=True)
    return (1.0 - learn_rate * decay_rate) * weights - learn_rate * back


def local(n, c, gradients, momentum, weights):
    new_momentum = hold_rate * momentum + gradients
    if weights.shape[1] % 8 == 0:
        new_weights = exchange_in_kernel(n, c, new_momentum, weights)
    else:
        new_weights = exchange_in_xla(new_momentum, weights)
    return (new_weights, new_momentum)


def solution(mesh):
    placed = (P(None, "rows", "cols"), P(None, "rows", "cols"), P(None, "rows", "cols"))
    return jax.shard_map(
        functools.partial(local, mesh.shape["rows"], mesh.shape["cols"]),
        mesh=mesh,
        in_specs=placed,
        out_specs=(P(None, "rows", "cols"), P(None, "rows", "cols")),
        check_vma=False,
    )
```

time: 178 us -> 103 us (0.58)
  the two profiles are of different devices: /device:TPU:0 before, /device:TPU:15 now
where the time goes in v1:
time: 103 us
  Pallas kernels  98.2 us (95%)
  other arithmetic  2.98 us (3%)
  local copies, waits for them, and re-layouts  1.33 us (1%)
    pallas_call x1, Pallas kernels, exchange_in_kernel(): pl.pallas_call(functools.partial(kernel, n, c), out_shape=jax.ShapeDtypeS...  98.2 us
    add x1, other arithmetic, local(): new_momentum = hold_rate * momentum + gradients  2.98 us

profile of v1, /device:TPU:15, one launch (start us, length us, event | category | flops | bytes accessed | tf_op | source)
XLA Modules:
  0.0 103.2 jit_solution(16598972646776861431)
XLA Ops:
  0.6 0.0 copy-start.1
  0.6 3.0 %multiply_add_fusion = f32[32,16,1024]{2,1,0:T(8,128)S(1)} fusion(f32[32,16,1024]{2,1,0:T(8,128)} %param.3, f32[32,16,1024]{2,1,0:T(8,128)} %param.4), kind=kLoop, calls=%fused_computation | loop fusion | flops 1048576 | bytes 6291456 | tf_op jit(solution)/shard_map/add | solution.py:212
  3.6 0.0 copy-start
  3.6 0.0 copy-done.1
  3.6 98.2 %shard_map.50 = f32[8,4,16,1024]{3,2,1,0:T(8,128)S(1)} custom-call(f32[8,4,16,1024]{3,2,1,0:T(8,128)S(1)} %bitcast.3, f32[8,4,16,1024]{3,2,1,0:T(8,128)S(1)} %bitcast.5), custom_call_target="tpu_custom_call" | custom-call | tf_op jit(solution)/shard_map/pallas_call | solution.py:164
  101.9 0.0 copy-done
  101.9 1.3 %copy.6 = f32[32,16,1024]{2,1,0:T(8,128)} copy(f32[32,16,1024]{2,1,0:T(8,128)S(1)} %bitcast.4) | data formatting | bytes 4194304
Async XLA Ops:
  0.6 3.0 %copy-start.1 = (f32[32,16,1024]{2,1,0:T(8,128)S(1)}, f32[32,16,1024]{2,1,0:T(8,128)}, u32[]{:S(2)}) copy-start(f32[32,16,1024]{2,1,0:T(8,128)} %param.5) | copy-start | bytes 6291460
  3.6 98.2 %copy-start = (f32[32,16,1024]{2,1,0:T(8,128)}, f32[32,16,1024]{2,1,0:T(8,128)S(1)}, u32[]{:S(2)}) copy-start(f32[32,16,1024]{2,1,0:T(8,128)S(1)} %multiply_add_fusion) | copy-start | bytes 6291460
